TPU v7x, 32 devices: a whole 2x2x4 slice. The times are simulated.
32 devices in a mesh: gx: 4 (over z), gy: 2 (over y), gz: 4 (over x, core).
Axes of the slice: x: 2, y: 2, z: 4, core: 2. Of those that a mesh axis runs over, the one named last changes fastest.
Arguments:
- state: float32 [9, 64, 32, 512], P(None, 'gx', 'gy', 'gz'), may hold values from 0 to 1
- mobility: float32 [8], replicated, may hold values from 0.5 to 2
- seeds: int32 [2, 2, 64, 32], replicated, may hold values from 0 to 8
- frame_shifts: int32 [2], replicated, may hold values from 0 to 2, as said below
Outputs:
- state_out: float32 [9, 64, 32, 512], P(None, 'gx', 'gy', 'gz')
Inputs may be any that keep to these rules, and one draw needn't show every extreme that they name: A value of 8 seeds no grain in that cell. `frame_shifts`: the frame advances 2 planes in at least one step and stays in place in at least one other.
All inputs are finite; a program needn't handle non-finite values.
Results may differ from a plain program's by a relative error of at most 0.0001.
Values sent between devices are 32-bit elements; how exact they have to be, the bound alone decides.
No kernel may reach another device: no remote copies, remote signals or barrier semaphores. Data moves between devices by JAX's collectives and lax.ppermute only.
A program may use at most 64 MiB of HBM per device.

v0:
```python
import functools
import math

import jax
import jax.numpy as jnp
from jax import lax
from jax.experimental import pallas as pl
from jax.experimental.pallas import tpu as pltpu
from jax.sharding import PartitionSpec as P


step_rate = 0.1
stiffness = 0.7
coupling = 0.5
diffusion = 0.14
rejection = 0.5
nucleus = 0.3
melt_solute = 1.0

TILE = 8
LANES = 128
REACH = 2
GROUP = 6
SHARE = 4
TRIO = 3
UNROLL = 16

VMEM = pl.BlockSpec(memory_space=pltpu.VMEM)
SMEM = pl.BlockSpec(memory_space=pltpu.SMEM)


def iota(shape, axis):
    return lax.broadcasted_iota(jnp.int32, shape, axis)


def is_even():
    return lax.rem(lax.axis_index("gx"), 2) == 0


def group_and_slot(ahead=0):
    lane = iota((1, LANES), 1) + ahead
    slot = lax.shift_right_logical(lane * 43, 8)
    return slot, lane - slot * GROUP


def edge_tile(ref, g, x):
    rows = ref.shape[2]
    low = ref[g, x, 0:TILE]
    high = ref[g, x, rows - TILE : rows]
    return jnp.where(iota((TILE, LANES), 0) < TILE // 2, low, high)


def corner_rows(k):
    row = iota((TILE, LANES), 0)
    return (row == 2 * k) | (row == (2 * k + TILE - 1) % TILE)


def outer_face_kernel(state, face, sem):
    start = jnp.where(is_even(), 0, state.shape[1] - REACH)
    copy = pltpu.make_async_copy(state.at[:, pl.ds(start, REACH)], face, sem)
    copy.start()
    copy.wait()


def rims_kernel(state, face_a, rows, corner_a, corner_b):
    fields, width = state.shape[:2]
    even = is_even()
    face_a[...] = state[:, pl.ds(jnp.where(even, width - REACH, 0), REACH)]
    row = iota((TILE, LANES), 0)
    outer = (row < REACH) | (row >= TILE - REACH)
    for g in range(fields):
        for pair in range(width // 2):
            first = edge_tile(state, g, 2 * pair)
            second = edge_tile(state, g, 2 * pair + 1)
            rows[g, pair] = jnp.where(outer, first, pltpu.roll(second, TILE // 2, 0))
    near_a = jnp.where(even, width - 1, 0)
    near_b = jnp.where(even, 0, width - 1)
    for corner, x in ((corner_a, near_a), (corner_b, near_b)):
        for t in range(corner.shape[0]):
            held = None
            for k in range(SHARE):
                g = t * SHARE + k
                if g < fields:
                    tile = edge_tile(state, g, x)
                    if k:
                        tile = jnp.where(corner_rows(k), pltpu.roll(tile, 2 * k, 0), held)
                    held = tile
            corner[t] = held


def bottom_mask(active):
    return jnp.where((iota((1, LANES), 1) == REACH) & active, 0.0, 1.0)


def along(p, mask):
    return pltpu.roll(p, 1, 1) * mask + pltpu.roll(p, LANES - 1, 1)


def heights(length, place, shift):
    span = float(length * lax.axis_size("gz"))
    zpos = (lax.axis_index("gz") * length + place).astype(jnp.float32) - shift
    return 1.0 - 2.0 * (zpos + 0.5) / span


def unpack_table(table):
    grains = table.shape[0] - TILE
    return [table[g : g + 1] for g in range(grains)], table[grains : grains + 1]


def step_of(center, sums, theta, speeds):
    grains = len(center) - 1
    return relax(center[:grains], center[grains], sums[:grains], sums[grains], theta, speeds)


def early_mask(first_shift):
    return bottom_mask((lax.axis_index("gz") == 0) & (first_shift > 0))


def slot_shift(slot):
    return (slot * GROUP + REACH) % LANES


def prepare_kernel(state, seeds, mobility, shifts, part, outer, own, below, marks, table, *sums):
    fields, width, height, length = state.shape
    rows = height + TILE
    total_x, total_y = seeds.shape[2:]
    slot, place = group_and_slot()
    ahead, _ = group_and_slot(1)
    mask = early_mask(shifts[0])
    lane = iota((1, LANES), 1)
    moved_by = jnp.broadcast_to(shifts[0].astype(jnp.float32), (TILE, LANES))
    theta = heights(length, lane, moved_by[0:1])
    speeds = [step_rate * mobility[g] for g in range(fields - 1)]
    for g, speed in enumerate(speeds):
        table[g : g + 1] = jnp.broadcast_to(speed, (1, LANES))
    table[fields - 1 : fields - 1 + TILE] = moved_by
    flat = state.reshape(fields * width * height, LANES)

    def lateral(g, x):
        start = (g * width + x) * height
        total = state[g, x - 1] + state[g, x + 1]
        return total + flat[start - 1 : start - 1 + height] + flat[start + 1 : start + 1 + height]

    for g in range(fields):
        sums[1][g] = along(state[g, 1], mask)
        outer[g, 0] = along(state[g, 0], mask)
        outer[g, 1] = along(state[g, width - 1], mask)
        below[g] = jnp.zeros((height, LANES), jnp.float32)
        own[g] = jnp.zeros((height, LANES), jnp.float32)
    for x in range(width):
        now, after = sums[x % 2], sums[1 - x % 2]
        for g in range(fields):
            moved = pltpu.roll(state[g, x], slot_shift(x + REACH), 1)
            own[g] = jnp.where(slot == x + REACH, moved, own[g])
            if 1 < x:
                moved = pltpu.roll(part[g, x - 2], slot_shift(x - 1 + REACH), 1)
                below[g] = jnp.where(ahead == x - 1 + REACH, moved, below[g])
        if 0 < x < width - 1:
            center = [state[g, x] for g in range(fields)]
            around = [lambda g=g: lateral(g, x) + now[g] for g in range(fields)]
            fresh = step_of(center, around, theta, speeds)
            for g in range(fields):
                part[g, x - 1] = fresh[g]
                if x + 1 < width - 1:
                    after[g] = along(state[g, x + 1], mask)

    step = jnp.where(shifts[0] > 0, 0, 1)
    row_y = iota((rows, total_y), 0)
    y = jnp.where(row_y >= height + TILE // 2, row_y - rows, row_y) + lax.axis_index("gy") * height
    y = jnp.where(y < 0, y + total_y, y)
    y = jnp.where(y >= total_y, y - total_y, y)
    pick_y = jnp.where(iota((rows, total_y), 1) == y, 1.0, 0.0)
    x = slot - REACH + lax.axis_index("gx") * width
    x = jnp.where(x < 0, x + total_x, x)
    x = jnp.where(x >= total_x, x - total_x, x)
    total = jnp.zeros((rows, LANES), jnp.float32)
    for k in range(REACH):
        chosen = seeds[step, k].astype(jnp.float32)
        across = lax.dot_general(
            pick_y, chosen, (((1,), (1,)), ((), ())), preferred_element_type=jnp.float32
        )
        pick_x = jnp.where((iota((total_x, LANES), 0) == x) & (place == REACH + k), 1.0, 0.0)
        total = total + jnp.dot(across, pick_x, preferred_element_type=jnp.float32)
    marks[...] = total


class Halo:
    def __init__(self, merged, face_a, face_b, rest):
        count = 1 if merged else 2
        self.merged = merged
        self.faces = (face_a, face_b)
        self.rows = rest[:count]
        self.corners = (rest[count : 2 * count], rest[2 * count : 3 * count])
        self.even = is_even()

    def both(self, refs, index):
        if self.merged:
            return refs[0][index]
        upper = iota((TILE, LANES), 0) < TILE // 2
        return jnp.where(upper, refs[0][index], refs[1][index])

    def face(self, g, side, n):
        a, b = (ref[g, n] for ref in self.faces)
        return jnp.where(self.even, a, b) if side else jnp.where(self.even, b, a)

    def pair(self, g, n):
        tile = self.both(self.rows, (g, n))
        return tile, pltpu.roll(tile, TILE // 2, 0)

    def corner(self, g, side):
        t, k = g // SHARE, g % SHARE
        a, b = (self.both(refs, (t,)) for refs in self.corners)
        tile = jnp.where(self.even, a, b) if side else jnp.where(self.even, b, a)
        return pltpu.roll(tile, TILE - 2 * k, 0) if k else tile


def slab_kernel(merged, own, face_a, face_b, *rest):
    slab, message = rest[-2:]
    halo = Halo(merged, face_a, face_b, rest[:-2])
    fields, height = own.shape[:2]
    width = 2 * halo.rows[0].shape[1]
    slot, place = group_and_slot()
    row = iota((TILE, LANES), 0)
    for g in range(fields):
        held = own[g]
        for side in range(2):
            for n in range(REACH):
                where = n + side * (width + REACH)
                moved = pltpu.roll(halo.face(g, side, n), slot_shift(where), 1)
                held = jnp.where(slot == where, moved, held)
        slab[g, 0:height] = held
        tiles = [(REACH - 1, halo.corner(g, 0)), (width + REACH, halo.corner(g, 1))]
        for n in range(width // 2):
            first, second = halo.pair(g, n)
            tiles += [(2 * n + REACH, first), (2 * n + 1 + REACH, second)]
        held = jnp.zeros((TILE, LANES), jnp.float32)
        for where, tile in tiles:
            held = jnp.where(slot == where, pltpu.roll(tile, slot_shift(where), 1), held)
        slab[g, height : height + TILE] = held
    for t in range(message.shape[0]):
        a, b, c = (slab[TRIO * t + n] for n in range(TRIO))
        a = jnp.where(place < REACH, pltpu.roll(c, LANES - REACH, 1), a)
        b = jnp.where(place < REACH, pltpu.roll(c, LANES - 2 * REACH, 1), b)
        message[t, 0:height] = a[0:height]
        message[t, height : 2 * height] = b[0:height]
        message[t, 2 * height : 2 * height + TILE] = jnp.where(
            (row < REACH) | (row >= TILE - REACH),
            a[height:],
            pltpu.roll(b[height:], TILE // 2, 0),
        )


def relax(phases, solute, sums, solute_sum, theta, speeds):
    squares = phases[0] * phases[0]
    for phase in phases[1:]:
        squares = squares + phase * phase
    excess = (theta - coupling * solute) - squares
    fresh = []
    fresh_squares = None
    for g, phase in enumerate(phases):
        speed = speeds[g]
        rate = speed * excess + (1.0 - 6.0 * stiffness * speed)
        new = phase * rate + (stiffness * speed) * sums[g]()
        fresh.append(new)
        fresh_squares = new * new if fresh_squares is None else fresh_squares + new * new
    kept = (1.0 - 6.0 * diffusion) - rejection * (fresh_squares - squares)
    fresh.append(solute * kept + diffusion * solute_sum())
    return fresh


def bulk_kernel(merged, state, part, outer, below, table, face_a, face_b, *rest):
    done, lower, first, edge, edge_sum, edge_new, beyond = rest[-11:-4]
    sums, pending = rest[-4:-2], rest[-2:]
    halo = Halo(merged, face_a, face_b, rest[:-11])
    fields, width, height, length = state.shape
    top = height + TILE
    unroll = math.gcd(width, UNROLL)
    chunk = next(c for c in (3, 2, 1) if (width + 2) % c == 0)
    ahead, _ = group_and_slot(1)
    speeds, first_shift = unpack_table(table)
    lane = iota((1, LANES), 1)
    own = slice(TILE, TILE + height)
    row = iota((TILE, LANES), 0)
    half = row < TILE // 2
    mask_first = early_mask(first_shift)
    theta_first = heights(length, lane, first_shift)

    def plane(g, x):
        if 0 <= x < width:
            return state[g, x]
        return halo.face(g, 0, x + REACH) if x < 0 else halo.face(g, 1, x - width)

    def fold(p, rim):
        low, high = p[0:TILE], p[height - TILE : height]
        upper = pltpu.roll(jnp.where(half, rim, high), REACH, 0)
        under = pltpu.roll(jnp.where(half, low, rim), TILE - REACH, 0)
        return jnp.where(half, upper, under)

    for g in range(fields):
        for n in range(width // 2):
            for x, rim in zip((2 * n, 2 * n + 1), halo.pair(g, n)):
                edge[g, x + REACH] = fold(state[g, x], rim)
        for side, x in ((0, -1), (1, width)):
            edge[g, x + REACH] = fold(plane(g, x), halo.corner(g, side))
            beyond[g, side] = along(plane(g, x), mask_first)
        for x in (-REACH, width + REACH - 1):
            p = plane(g, x)
            edge[g, x + REACH] = fold(p, p[0:TILE])
        for x in range(1, width - 1):
            first[g, x + 1, own] = part[g, x - 1]
    for g in range(fields):
        for i in range(width + 2):
            edge_sum[g, i] = along(edge[g, i + 1], mask_first)

    for x in (-1, 0, width - 1, width):
        zsums, side = (outer, int(x > 0)) if 0 <= x < width else (beyond, int(x > 0))

        def around(g):
            center = plane(g, x)
            total = plane(g, x - 1) + plane(g, x + 1) + zsums[g, side]
            return total + pltpu.roll(center, 1, 0) + pltpu.roll(center, height - 1, 0)

        center = [plane(g, x) for g in range(fields)]
        parts = [functools.partial(around, g) for g in range(fields)]
        fresh = step_of(center, parts, theta_first, speeds)
        for g in range(fields):
            first[g, x + 1, own] = fresh[g]

    for i in range(0, width + 2, chunk):

        def tiles(ref, g, start):
            return jnp.concatenate([ref[g, start + t] for t in range(chunk)], axis=0)

        def turned(g, shift):
            return jnp.concatenate(
                [pltpu.roll(edge[g, i + 1 + t], shift, 0) for t in range(chunk)], axis=0
            )

        def around(g):
            total = tiles(edge, g, i) + tiles(edge, g, i + 2) + tiles(edge_sum, g, i)
            return total + turned(g, 1) + turned(g, TILE - 1)

        center = [tiles(edge, g, i + 1) for g in range(fields)]
        parts = [functools.partial(around, g) for g in range(fields)]
        fresh = step_of(center, parts, theta_first, speeds)
        for g in range(fields):
            for t in range(chunk):
                tile = fresh[g][t * TILE : (t + 1) * TILE]
                edge_new[g, i + t] = tile
                first[g, i + t, top - 1 : top + 1] = tile[1:3]
                first[g, i + t, TILE - 1 : TILE + 1] = tile[5:7]

    for g in range(fields):
        held = below[g]
        for x in (-1, 0, width - 1, width):
            moved = pltpu.roll(first[g, x + 1, own], slot_shift(x + REACH), 1)
            held = jnp.where(ahead == x + REACH, moved, held)
        rim = jnp.zeros((TILE, LANES), jnp.float32)
        for i in range(width + 2):
            moved = pltpu.roll(edge_new[g, i], slot_shift(i + 1), 1)
            rim = jnp.where(ahead == i + 1, moved, rim)
        forward, back = pltpu.roll(rim, REACH, 0), pltpu.roll(rim, TILE - REACH, 0)
        lower[g, 0:height] = held
        lower[g, 0:TILE] = jnp.where(row == 0, forward, held[0:TILE])
        lower[g, height - TILE : height] = jnp.where(
            row == TILE - 1, back, held[height - TILE : height]
        )
        lower[g, height : height + TILE] = jnp.where(half, back, forward)

    def lateral(g, x):
        total = first[g, x - 1, own] + first[g, x + 1, own]
        return total + first[g, x, TILE - 1 : top - 1] + first[g, x, TILE + 1 : top + 1]

    theta_second = heights(length, lane, float(REACH))
    mask_second = bottom_mask(lax.axis_index("gz") == 0)

    for g in range(fields):
        sums[0][g] = along(first[g, 1, own], mask_second)
        pending[1][g] = jnp.zeros((height, LANES), jnp.float32)

    def flush(held, x):
        for g in range(fields):
            done[g, x] = pltpu.roll(held[g], LANES - REACH, 1)

    @pl.loop(0, width // unroll)
    def _(block):
        for part in range(unroll):
            x = block * unroll + part
            now, after = part % 2, 1 - part % 2
            flush(pending[after], jnp.maximum(x - 1, 0))
            full = [first[g, x + 1, own] for g in range(fields)]
            parts = [lambda g=g: lateral(g, x + 1) + sums[now][g] for g in range(fields)]
            fresh = step_of(full, parts, theta_second, speeds)
            for g in range(fields):
                pending[now][g] = fresh[g]
                sums[after][g] = along(first[g, x + 2, own], mask_second)

    flush(pending[1], width - 1)


def crown_kernel(done, slab, above, lower, marks, table, out, whole, sems):
    fields, rows = slab.shape[:2]
    grains = fields - 1
    width, height, length = done.shape[1:]
    topmost = lax.axis_index("gz") == lax.axis_size("gz") - 1
    _, place = group_and_slot()
    speeds, first_shift = unpack_table(table)
    early = first_shift > 0

    def entering(g):
        if g == grains:
            return jnp.full((rows, LANES), melt_solute, jnp.float32)
        return jnp.where(marks[...] == float(g), nucleus, 0.0)

    below = (place == 0) | (place == GROUP - 1)
    planted = (place >= REACH) & (place < 2 * REACH)
    zero = jnp.zeros((rows, LANES), jnp.float32)

    def arrived(t):
        a, b = above[t, 0:height], above[t, height : 2 * height]
        rim = above[t, 2 * height : 2 * height + TILE]
        a = jnp.concatenate([a, rim], axis=0)
        b = jnp.concatenate([b, pltpu.roll(rim, TILE // 2, 0)], axis=0)
        c = jnp.where(
            place < 2 * REACH, pltpu.roll(a, REACH, 1), pltpu.roll(b, 2 * REACH, 1)
        )
        return a, b, c

    def around(p):
        total = pltpu.roll(p, GROUP, 1) + pltpu.roll(p, LANES - GROUP, 1)
        total = total + pltpu.roll(p, 1, 0) + pltpu.roll(p, rows - 1, 0)
        return total + pltpu.roll(p, 1, 1) + pltpu.roll(p, LANES - 1, 1)

    def advance(ps, theta):
        sums = [functools.partial(around, p) for p in ps]
        return relax(ps[:grains], ps[grains], sums[:grains], sums[grains], theta, speeds)

    before = []
    upper = [p for t in range(above.shape[0]) for p in arrived(t)]
    for g in range(fields):
        high = jnp.where(topmost, jnp.where(planted & early, entering(g), zero), upper[g])
        before.append(jnp.where(place < REACH, slab[g], high))
    middle = advance(before, heights(length, length - REACH + place, first_shift))
    after = []
    for g in range(fields):
        value = middle[g]
        value = jnp.where(topmost & jnp.logical_not(early) & planted, entering(g), value)
        value = jnp.where(topmost & (place >= 2 * REACH), 0.0, value)
        after.append(jnp.where(below, lower[g], value))
    final = advance(after, heights(length, length - REACH + place, float(REACH)))

    top = iota((1, LANES), 1) >= LANES - 2 * REACH
    copies = []
    for g in range(fields):
        cut = final[g][0:height]
        for x in range(width):
            shift = (LANES - 2 * REACH - (x + REACH) * GROUP) % LANES
            whole[g, x] = jnp.where(top, pltpu.roll(cut, shift, 1), done[g, x])
        copy = pltpu.make_async_copy(whole.at[g], out.at[g], sems.at[g])
        copy.start()
        copies.append(copy)
    for copy in copies:
        copy.wait()


def shape(*dims):
    return jax.ShapeDtypeStruct(dims, jnp.float32)


def call(kernel, outs, inputs, cost, specs=None, outs_specs=None, scratch=(), grant=24 << 20):
    return pl.pallas_call(
        kernel,
        out_shape=outs,
        in_specs=specs or [VMEM] * len(inputs),
        out_specs=outs_specs or jax.tree.map(lambda _: VMEM, outs),
        scratch_shapes=list(scratch),
        cost_estimate=pl.CostEstimate(flops=cost, bytes_accessed=cost, transcendentals=0),
        compiler_params=pltpu.CompilerParams(vmem_limit_bytes=grant),
    )(*inputs)


def shards(state, mobility, seeds, frame_shifts):
    fields, width, height, length = state.shape
    count_x, count_y, count_z = (lax.axis_size(a) for a in ("gx", "gy", "gz"))
    merged = count_y == 2
    rows = height + TILE
    groups = -(-fields // SHARE)
    whole = shape(fields, width, height, length)
    packed = shape(fields, rows, length)

    def partner(i, kind):
        return (i + 1) % count_x if (i % 2 == 0) == (kind == 0) else (i - 1) % count_x

    def swap(value, pairs):
        return lax.ppermute(value, "gx", pairs + [(j, i) for i, j in pairs])

    toward = [-1] if merged else [-1, 1]

    def diagonal(value, kind):
        return [
            lax.ppermute(
                value,
                ("gx", "gy"),
                [
                    (i * count_y + j, partner(i, kind) * count_y + (j + d) % count_y)
                    for i in range(count_x)
                    for j in range(count_y)
                ],
            )
            for d in toward
        ]

    face = shape(fields, REACH, height, length)
    face_b = call(
        outer_face_kernel,
        face,
        [pltpu.with_memory_space_constraint(state, pltpu.HBM)],
        100000,
        specs=[pl.BlockSpec(memory_space=pltpu.HBM)],
        scratch=[pltpu.SemaphoreType.DMA(())],
    )
    got_b = swap(face_b, [(i, (i + 1) % count_x) for i in range(1, count_x, 2)])
    face_a, edge, corner_a, corner_b = call(
        rims_kernel,
        [
            face,
            shape(fields, width // 2, TILE, length),
            shape(groups, TILE, length),
            shape(groups, TILE, length),
        ],
        [state],
        100000,
    )
    near = [
        lax.ppermute(edge, "gy", [(j, (j + d) % count_y) for j in range(count_y)])
        for d in toward
    ]
    got_a = swap(face_a, [(i, i + 1) for i in range(0, count_x, 2)])
    far_b = diagonal(corner_b, 1)
    far_a = diagonal(corner_a, 0)
    sides = shape(fields, 2, height, length)
    flat = shape(fields, height, length)
    lines = pltpu.VMEM((fields, height, length), jnp.float32)
    part, outer, own, below, marks, table = call(
        prepare_kernel,
        [
            shape(fields, width - 2, height, length),
            sides,
            flat,
            flat,
            shape(rows, length),
            shape(fields - 1 + TILE, length),
        ],
        [state, seeds, mobility, frame_shifts],
        5000000,
        specs=[VMEM, VMEM, SMEM, SMEM],
        scratch=[lines, lines],
    )
    halo = [got_a, got_b, *near, *far_a, *far_b]
    slab, message = call(
        functools.partial(slab_kernel, merged),
        [packed, shape(fields // TRIO, 2 * height + TILE, length)],
        [own, *halo],
        100000,
    )
    above = lax.ppermute(message, "gz", [(k, (k - 1) % count_z) for k in range(count_z)])
    done, lower = call(
        functools.partial(bulk_kernel, merged),
        [whole, packed],
        [state, part, outer, below, table, *halo],
        20000000,
        scratch=[
            pltpu.VMEM((fields, width + 2, rows + TILE, length), jnp.float32),
            pltpu.VMEM((fields, width + 2 * REACH, TILE, length), jnp.float32),
            pltpu.VMEM((fields, width + 2, TILE, length), jnp.float32),
            pltpu.VMEM((fields, width + 2, TILE, length), jnp.float32),
            pltpu.VMEM((fields, 2, height, length), jnp.float32),
            lines,
            lines,
            lines,
            lines,
        ],
    )
    return call(
        crown_kernel,
        whole,
        [done, slab, above, lower, marks, table],
        100000,
        outs_specs=pl.BlockSpec(memory_space=pltpu.HBM),
        scratch=[
            pltpu.VMEM((fields, width, height, length), jnp.float32),
            pltpu.SemaphoreType.DMA((fields,)),
        ],
    )


def solution(mesh):
    placed = (P(None, "gx", "gy", "gz"), P(), P(), P())
    return jax.shard_map(
        shards, mesh=mesh, in_specs=placed, out_specs=P(None, "gx", "gy", "gz"), check_vma=False
    )
```

profile of v0, /device:TPU:1, one launch (start us, length us, event | category | flops | bytes accessed | tf_op | source)
XLA Modules:
  0.0 22.2 jit_solution(10765937975717107679)
XLA Ops:
  0.0 0.0 copy-start
  0.0 1.3 %copy-done = f32[9,16,16,128]{3,2,1,0:T(8,128)S(1)} copy-done((f32[9,16,16,128]{3,2,1,0:T(8,128)S(1)}, f32[9,16,16,128]{3,2,1,0:T(8,128)}, u32[]{:S(2)}) %copy-start) | copy-done | bytes 1179672
  1.3 0.0 copy-start.4
  1.3 0.0 copy-start.1
  1.3 0.0 copy-start.2
  1.3 0.0 copy-start.3
  1.3 0.1 shard_map.47
  1.4 2.1 %collective-permute-start.2 = (f32[9,8,8,128]{3,2,1,0:T(8,128)S(1)}, f32[9,8,8,128]{3,2,1,0:T(8,128)S(1)}, u32[]{:S(2)}, u32[]{:S(2)}) collective-permute-start(f32[9,8,8,128]{3,2,1,0:T(8,128)S(1)} %get-tuple-element.24), channel_id=1, source_target_pairs={{0,4},{4,0},{1,5},{5,1},{2,6},{6,2},{3,7},{7,3},{8,12},{12,8},{9,1... | collective-permute-start | bytes 884744 | tf_op jit(solution)/shard_map/ppermute | solution.py:535
  3.5 0.9 %shard_map.48 = f32[9,2,16,128]{3,2,1,0:T(8,128)S(1)} custom-call(f32[9,16,16,128]{3,2,1,0:T(8,128)} %state.7), custom_call_target="tpu_custom_call" | custom-call | flops 100000 | bytes 100000 | tf_op jit(solution)/shard_map/pallas_call | solution.py:471
  4.4 3.4 %collective-permute-start.1 = (f32[9,2,16,128]{3,2,1,0:T(8,128)S(1)}, f32[9,2,16,128]{3,2,1,0:T(8,128)S(1)}, u32[]{:S(2)}, u32[]{:S(2)}) collective-permute-start(f32[9,2,16,128]{3,2,1,0:T(8,128)S(1)} %shard_map.48), channel_id=1, source_target_pairs={{8,16},{24,0},{16,8},{0,24},{9,17},{25,1},{17,9},{1,25},{10,18},{2... | collective-permute-start | bytes 442376 | tf_op jit(solution)/shard_map/ppermute | solution.py:495
  7.8 0.0 collective-permute-start
  7.8 1.4 %collective-permute-start.3 = (f32[3,8,128]{2,1,0:T(8,128)S(1)}, f32[3,8,128]{2,1,0:T(8,128)S(1)}, u32[]{:S(2)}, u32[]{:S(2)}) collective-permute-start(f32[3,8,128]{2,1,0:T(8,128)S(1)} %get-tuple-element.25), channel_id=1, source_target_pairs={{0,12},{4,8},{8,4},{12,0},{16,28},{20,24},{24,20},{28,16},{1,13},{... | collective-permute-start | bytes 36872 | tf_op jit(solution)/shard_map/ppermute | solution.py:501
  9.2 1.0 %collective-permute-start.4 = (f32[3,8,128]{2,1,0:T(8,128)S(1)}, f32[3,8,128]{2,1,0:T(8,128)S(1)}, u32[]{:S(2)}, u32[]{:S(2)}) collective-permute-start(f32[3,8,128]{2,1,0:T(8,128)S(1)} %get-tuple-element.26), channel_id=1, source_target_pairs={{0,28},{4,24},{8,20},{12,16},{16,12},{20,8},{24,4},{28,0},{1,29},{... | collective-permute-start | bytes 36872 | tf_op jit(solution)/shard_map/ppermute | solution.py:501
  10.2 0.0 copy-done.4
  10.2 0.1 copy.5.seeds
  10.3 0.0 copy-done.1
  10.4 0.0 copy-done.2
  10.4 0.0 copy-done.3
  10.4 1.8 %shard_map.46 = (f32[9,14,16,128]{3,2,1,0:T(8,128)S(1)}, f32[9,2,16,128]{3,2,1,0:T(8,128)S(1)}, f32[9,16,128]{2,1,0:T(8,128)S(1)}, f32[9,16,128]{2,1,0:T(8,128)S...) custom-call(f32[9,16,16,128]{3,2,1,0:T(8,128)S(1)} %copy-done.1, s32[2,2,64,32]{3,2,1,0:T(8,128)S(1)} %copy.5.seeds, ...), custom_call_target="tpu_custom_call" | custom-call | flops 5000000 | bytes 5000000 | tf_op jit(solution)/shard_map/pallas_call | solution.py:471
  12.2 2.9 %collective-permute-done.3.rest_1_ = f32[3,8,128]{2,1,0:T(8,128)S(1)} collective-permute-done((f32[3,8,128]{2,1,0:T(8,128)S(1)}, f32[3,8,128]{2,1,0:T(8,128)S(1)}, u32[]{:S(2)}, u32[]{:S(2)}) %collective-permute-start.3) | collective-permute-done | bytes 12320 | tf_op jit(solution)/shard_map/ppermute | solution.py:501
  15.1 0.0 collective-permute-done.4.rest_2_
  15.1 0.0 collective-permute-done.1.face_b
  15.1 0.0 collective-permute-done.face_a
  15.1 0.0 collective-permute-done.2.rest_0_
  15.1 0.4 %shard_map.50 = (f32[9,24,128]{2,1,0:T(8,128)S(1)}, f32[3,40,128]{2,1,0:T(8,128)S(1)}) custom-call(f32[9,16,128]{2,1,0:T(8,128)S(1)} %get-tuple-element.28.own, f32[9,2,16,128]{3,2,1,0:T(8,128)S(1)} %collective-permute-done.face_a, f32[9,2,16,128]{3,2,1,0:T(8,128)S(1)} %collective-permute-done.1.face_b, f32[9,8,8,128]{3,2,1,0:T(8,128)S(1)} %collective-permute-done.2.rest_0_, ...), custom_call_target="tpu_custom_call" | custom-call | flops 100000 | bytes 100000 | tf_op jit(solution)/shard_map/pallas_call | solution.py:471
  15.5 2.3 %collective-permute-start.5 = (f32[3,40,128]{2,1,0:T(8,128)S(1)}, f32[3,40,128]{2,1,0:T(8,128)S(1)}, u32[]{:S(2)}, u32[]{:S(2)}) collective-permute-start(f32[3,40,128]{2,1,0:T(8,128)S(1)} %get-tuple-element.30), channel_id=1, source_target_pairs={{0,3},{1,0},{2,1},{3,2},{4,7},{5,4},{6,5},{7,6},{8,11},{9,8},{10,9... | collective-permute-start | bytes 184328 | tf_op jit(solution)/shard_map/ppermute | solution.py:566
  17.8 1.9 %shard_map.49 = (f32[9,16,16,128]{3,2,1,0:T(8,128)S(1)}, f32[9,24,128]{2,1,0:T(8,128)S(1)}) custom-call(f32[9,16,16,128]{3,2,1,0:T(8,128)S(1)} %copy-done.1, f32[9,14,16,128]{3,2,1,0:T(8,128)S(1)} %get-tuple-element.19.part, f32[9,2,16,128]{3,2,1,0:T(8,128)S(1)} %get-tuple-element.20.outer, f32[9,16,128]{2,1,0:T(8,128)S(1)} %get-tuple-element.21.below, ...), custom_call_target="tpu_custom_call" | custom-call | flops 20000000 | bytes 20000000 | tf_op jit(solution)/shard_map/pallas_call | solution.py:471
  19.8 1.1 %collective-permute-done.5.above = f32[3,40,128]{2,1,0:T(8,128)S(1)} collective-permute-done((f32[3,40,128]{2,1,0:T(8,128)S(1)}, f32[3,40,128]{2,1,0:T(8,128)S(1)}, u32[]{:S(2)}, u32[]{:S(2)}) %collective-permute-start.5) | collective-permute-done | bytes 61472 | tf_op jit(solution)/shard_map/ppermute | solution.py:566
  20.8 1.4 %shard_map.51 = f32[9,16,16,128]{3,2,1,0:T(8,128)} custom-call(f32[9,16,16,128]{3,2,1,0:T(8,128)S(1)} %get-tuple-element.27.done, f32[9,24,128]{2,1,0:T(8,128)S(1)} %get-tuple-element.29.slab, f32[3,40,128]{2,1,0:T(8,128)S(1)} %collective-permute-done.5.above, f32[9,24,128]{2,1,0:T(8,128)S(1)} %get-tuple-element.31.lower, ...), custom_call_target="tpu_custom_call" | custom-call | flops 100000 | bytes 100000 | tf_op jit(solution)/shard_map/pallas_call | solution.py:471
Async XLA Ops:
  0.0 1.3 %copy-start = (f32[9,16,16,128]{3,2,1,0:T(8,128)S(1)}, f32[9,16,16,128]{3,2,1,0:T(8,128)}, u32[]{:S(2)}) copy-start(f32[9,16,16,128]{3,2,1,0:T(8,128)} %state.7) | copy-start | bytes 3538948
  1.3 9.0 %copy-start.4 = (s32[2,2,64,32]{2,3,1,0:T(8,128)S(1)}, s32[2,2,64,32]{2,3,1,0:T(8,128)}, u32[]{:S(2)}) copy-start(s32[2,2,64,32]{2,3,1,0:T(8,128)} %param.6) | copy-start | bytes 98308
  1.3 9.1 %copy-start.1 = (f32[9,16,16,128]{3,2,1,0:T(8,128)S(1)}, f32[9,16,16,128]{3,2,1,0:T(8,128)}, u32[]{:S(2)}) copy-start(f32[9,16,16,128]{3,2,1,0:T(8,128)} %state.7) | copy-start | bytes 3538948
  1.3 9.1 %copy-start.2 = (f32[8]{0:T(128)S(1)}, f32[8]{0:T(128)}, u32[]{:S(2)}) copy-start(f32[8]{0:T(128)} %mobility.1) | copy-start | bytes 100
  1.3 9.1 %copy-start.3 = (s32[2]{0:T(128)S(1)}, s32[2]{0:T(128)}, u32[]{:S(2)}) copy-start(s32[2]{0:T(128)} %shifts.1) | copy-start | bytes 28
  1.4 13.8 %collective-permute-start.2 = (f32[9,8,8,128]{3,2,1,0:T(8,128)S(1)}, f32[9,8,8,128]{3,2,1,0:T(8,128)S(1)}, u32[]{:S(2)}, u32[]{:S(2)}) collective-permute-start(f32[9,8,8,128]{3,2,1,0:T(8,128)S(1)} %get-tuple-element.24), channel_id=1, source_target_pairs={{0,4},{4,0},{1,5},{5,1},{2,6},{6,2},{3,7},{7,3},{8,12},{12,8},{9,1... | collective-permute-start | bytes 884744 | tf_op jit(solution)/shard_map/ppermute | solution.py:535
  4.4 10.7 %collective-permute-start.1 = (f32[9,2,16,128]{3,2,1,0:T(8,128)S(1)}, f32[9,2,16,128]{3,2,1,0:T(8,128)S(1)}, u32[]{:S(2)}, u32[]{:S(2)}) collective-permute-start(f32[9,2,16,128]{3,2,1,0:T(8,128)S(1)} %shard_map.48), channel_id=1, source_target_pairs={{8,16},{24,0},{16,8},{0,24},{9,17},{25,1},{17,9},{1,25},{10,18},{2... | collective-permute-start | bytes 442376 | tf_op jit(solution)/shard_map/ppermute | solution.py:495
  7.8 7.3 %collective-permute-start = (f32[9,2,16,128]{3,2,1,0:T(8,128)S(1)}, f32[9,2,16,128]{3,2,1,0:T(8,128)S(1)}, u32[]{:S(2)}, u32[]{:S(2)}) collective-permute-start(f32[9,2,16,128]{3,2,1,0:T(8,128)S(1)} %get-tuple-element.23), channel_id=1, source_target_pairs={{0,8},{16,24},{8,0},{24,16},{1,9},{17,25},{9,1},{25,17},{2,10},{18... | collective-permute-start | bytes 442376 | tf_op jit(solution)/shard_map/ppermute | solution.py:495
  7.8 7.3 %collective-permute-start.3 = (f32[3,8,128]{2,1,0:T(8,128)S(1)}, f32[3,8,128]{2,1,0:T(8,128)S(1)}, u32[]{:S(2)}, u32[]{:S(2)}) collective-permute-start(f32[3,8,128]{2,1,0:T(8,128)S(1)} %get-tuple-element.25), channel_id=1, source_target_pairs={{0,12},{4,8},{8,4},{12,0},{16,28},{20,24},{24,20},{28,16},{1,13},{... | collective-permute-start | bytes 36872 | tf_op jit(solution)/shard_map/ppermute | solution.py:501
  9.2 5.9 %collective-permute-start.4 = (f32[3,8,128]{2,1,0:T(8,128)S(1)}, f32[3,8,128]{2,1,0:T(8,128)S(1)}, u32[]{:S(2)}, u32[]{:S(2)}) collective-permute-start(f32[3,8,128]{2,1,0:T(8,128)S(1)} %get-tuple-element.26), channel_id=1, source_target_pairs={{0,28},{4,24},{8,20},{12,16},{16,12},{20,8},{24,4},{28,0},{1,29},{... | collective-permute-start | bytes 36872 | tf_op jit(solution)/shard_map/ppermute | solution.py:501
  15.5 5.3 %collective-permute-start.5 = (f32[3,40,128]{2,1,0:T(8,128)S(1)}, f32[3,40,128]{2,1,0:T(8,128)S(1)}, u32[]{:S(2)}, u32[]{:S(2)}) collective-permute-start(f32[3,40,128]{2,1,0:T(8,128)S(1)} %get-tuple-element.30), channel_id=1, source_target_pairs={{0,3},{1,0},{2,1},{3,2},{4,7},{5,4},{6,5},{7,6},{8,11},{9,8},{10,9... | collective-permute-start | bytes 184328 | tf_op jit(solution)/shard_map/ppermute | solution.py:566
where the time goes:
time: 22.4 us; the launch traced here: 22.2 us
  starting transfers between devices  10.3 us (46%)
  Pallas kernels  6.51 us (29%)
  waiting for transfers between devices  3.98 us (18%)
  local copies, waits for them, and re-layouts  1.38 us (6%)
    pallas_call x6, Pallas kernels, call(): pl.pallas_call(kernel, out_shape=outs, in_specs=specs or [VMEM] * len(inp...  6.51 us
    ppermute x2, starting transfers between devices, swap(): return lax.ppermute(value, 'gx', pairs + [(j, i) for i, j in pairs])  3.39 us
    ppermute x2, waiting for transfers between devices, diagonal(): lax.ppermute(value, ('gx', 'gy'), [(i * count_y + j, partner(i, kind) * c...  2.92 us
    ppermute x2, starting transfers between devices, diagonal(): lax.ppermute(value, ('gx', 'gy'), [(i * count_y + j, partner(i, kind) * c...  2.44 us
    ppermute x1, starting transfers between devices, shards(): lax.ppermute(message, 'gz', [(k, (k - 1) % count_z) for k in range(count_...  2.33 us
    ppermute x1, starting transfers between devices, shards(): lax.ppermute(edge, 'gy', [(j, (j + d) % count_y) for j in range(count_y)])  2.12 us
    unnamed x11, local copies, waits for them, and re-layouts  1.38 us
    ppermute x1, waiting for transfers between devices, shards(): lax.ppermute(message, 'gz', [(k, (k - 1) % count_z) for k in range(count_...  1.06 us
  transfers between devices with their start and end apart: 6, of which 2 were waited for; matrix products, arithmetic and copies ran while one was open for 0% of the time, Pallas kernels for 21%

commit v1 on v0

--- a/solution.py
+++ b/solution.py
@@ -57,9 +57,14 @@
 
 def outer_face_kernel(state, face, sem):
     start = jnp.where(is_even(), 0, state.shape[1] - REACH)
-    copy = pltpu.make_async_copy(state.at[:, pl.ds(start, REACH)], face, sem)
-    copy.start()
-    copy.wait()
+    copies = [
+        pltpu.make_async_copy(state.at[g, pl.ds(start, REACH)], face.at[g], sem.at[g])
+        for g in range(state.shape[0])
+    ]
+    for copy in copies:
+        copy.start()
+    for copy in copies:
+        copy.wait()
 
 
 def rims_kernel(state, face_a, rows, corner_a, corner_b):
@@ -517,7 +522,7 @@
         [pltpu.with_memory_space_constraint(state, pltpu.HBM)],
         100000,
         specs=[pl.BlockSpec(memory_space=pltpu.HBM)],
-        scratch=[pltpu.SemaphoreType.DMA(())],
+        scratch=[pltpu.SemaphoreType.DMA((fields,))],
     )
     got_b = swap(face_b, [(i, (i + 1) % count_x) for i in range(1, count_x, 2)])
     face_a, edge, corner_a, corner_b = call(

time: 22.4 us -> 22.5 us (level)
  no operation moved by 1% of the time
where the time goes in v1:
time: 22.5 us; the launch traced here: 22.2 us
  starting transfers between devices  10.3 us (46%)
  Pallas kernels  6.52 us (29%)
  waiting for transfers between devices  3.93 us (17%)
  local copies, waits for them, and re-layouts  1.38 us (6%)
    pallas_call x6, Pallas kernels, call(): pl.pallas_call(kernel, out_shape=outs, in_specs=specs or [VMEM] * len(inp...  6.52 us
    ppermute x2, starting transfers between devices, swap(): return lax.ppermute(value, 'gx', pairs + [(j, i) for i, j in pairs])  3.39 us
    ppermute x2, waiting for transfers between devices, diagonal(): lax.ppermute(value, ('gx', 'gy'), [(i * count_y + j, partner(i, kind) * c...  2.86 us
    ppermute x2, starting transfers between devices, diagonal(): lax.ppermute(value, ('gx', 'gy'), [(i * count_y + j, partner(i, kind) * c...  2.44 us
    ppermute x1, starting transfers between devices, shards(): lax.ppermute(message, 'gz', [(k, (k - 1) % count_z) for k in range(count_...  2.38 us
    ppermute x1, starting transfers between devices, shards(): lax.ppermute(edge, 'gy', [(j, (j + d) % count_y) for j in range(count_y)])  2.12 us
    unnamed x11, local copies, waits for them, and re-layouts  1.38 us
    ppermute x1, waiting for transfers between devices, shards(): lax.ppermute(message, 'gz', [(k, (k - 1) % count_z) for k in range(count_...  1.06 us
  transfers between devices with their start and end apart: 6, of which 2 were waited for; matrix products, arithmetic and copies ran while one was open for 0% of the time, Pallas kernels for 21%

profile of v1, /device:TPU:1, one launch (start us, length us, event | category | flops | bytes accessed | tf_op | source)
XLA Modules:
  0.0 22.2 jit_solution(16698642141261899777)
XLA Ops:
  0.0 0.0 copy-start
  0.0 1.3 %copy-done = f32[9,16,16,128]{3,2,1,0:T(8,128)S(1)} copy-done((f32[9,16,16,128]{3,2,1,0:T(8,128)S(1)}, f32[9,16,16,128]{3,2,1,0:T(8,128)}, u32[]{:S(2)}) %copy-start) | copy-done | bytes 1179672
  1.3 0.0 copy-start.4
  1.3 0.0 copy-start.1
  1.3 0.0 copy-start.2
  1.3 0.0 copy-start.3
  1.3 0.1 shard_map.47
  1.4 2.1 %collective-permute-start.2 = (f32[9,8,8,128]{3,2,1,0:T(8,128)S(1)}, f32[9,8,8,128]{3,2,1,0:T(8,128)S(1)}, u32[]{:S(2)}, u32[]{:S(2)}) collective-permute-start(f32[9,8,8,128]{3,2,1,0:T(8,128)S(1)} %get-tuple-element.24), channel_id=1, source_target_pairs={{0,4},{4,0},{1,5},{5,1},{2,6},{6,2},{3,7},{7,3},{8,12},{12,8},{9,1... | collective-permute-start | bytes 884744 | tf_op jit(solution)/shard_map/ppermute | solution.py:540
  3.5 0.9 %shard_map.48 = f32[9,2,16,128]{3,2,1,0:T(8,128)S(1)} custom-call(f32[9,16,16,128]{3,2,1,0:T(8,128)} %state.7), custom_call_target="tpu_custom_call" | custom-call | flops 100000 | bytes 100000 | tf_op jit(solution)/shard_map/pallas_call | solution.py:476
  4.4 3.4 %collective-permute-start.1 = (f32[9,2,16,128]{3,2,1,0:T(8,128)S(1)}, f32[9,2,16,128]{3,2,1,0:T(8,128)S(1)}, u32[]{:S(2)}, u32[]{:S(2)}) collective-permute-start(f32[9,2,16,128]{3,2,1,0:T(8,128)S(1)} %shard_map.48), channel_id=1, source_target_pairs={{8,16},{24,0},{16,8},{0,24},{9,17},{25,1},{17,9},{1,25},{10,18},{2... | collective-permute-start | bytes 442376 | tf_op jit(solution)/shard_map/ppermute | solution.py:500
  7.8 0.0 collective-permute-start
  7.8 1.4 %collective-permute-start.3 = (f32[3,8,128]{2,1,0:T(8,128)S(1)}, f32[3,8,128]{2,1,0:T(8,128)S(1)}, u32[]{:S(2)}, u32[]{:S(2)}) collective-permute-start(f32[3,8,128]{2,1,0:T(8,128)S(1)} %get-tuple-element.25), channel_id=1, source_target_pairs={{0,12},{4,8},{8,4},{12,0},{16,28},{20,24},{24,20},{28,16},{1,13},{... | collective-permute-start | bytes 36872 | tf_op jit(solution)/shard_map/ppermute | solution.py:506
  9.2 1.0 %collective-permute-start.4 = (f32[3,8,128]{2,1,0:T(8,128)S(1)}, f32[3,8,128]{2,1,0:T(8,128)S(1)}, u32[]{:S(2)}, u32[]{:S(2)}) collective-permute-start(f32[3,8,128]{2,1,0:T(8,128)S(1)} %get-tuple-element.26), channel_id=1, source_target_pairs={{0,28},{4,24},{8,20},{12,16},{16,12},{20,8},{24,4},{28,0},{1,29},{... | collective-permute-start | bytes 36872 | tf_op jit(solution)/shard_map/ppermute | solution.py:506
  10.3 0.0 copy-done.4
  10.3 0.1 copy.5.seeds
  10.4 0.0 copy-done.1
  10.4 0.0 copy-done.2
  10.4 0.0 copy-done.3
  10.4 1.8 %shard_map.46 = (f32[9,14,16,128]{3,2,1,0:T(8,128)S(1)}, f32[9,2,16,128]{3,2,1,0:T(8,128)S(1)}, f32[9,16,128]{2,1,0:T(8,128)S(1)}, f32[9,16,128]{2,1,0:T(8,128)S...) custom-call(f32[9,16,16,128]{3,2,1,0:T(8,128)S(1)} %copy-done.1, s32[2,2,64,32]{3,2,1,0:T(8,128)S(1)} %copy.5.seeds, ...), custom_call_target="tpu_custom_call" | custom-call | flops 5000000 | bytes 5000000 | tf_op jit(solution)/shard_map/pallas_call | solution.py:476
  12.2 2.9 %collective-permute-done.3.rest_1_ = f32[3,8,128]{2,1,0:T(8,128)S(1)} collective-permute-done((f32[3,8,128]{2,1,0:T(8,128)S(1)}, f32[3,8,128]{2,1,0:T(8,128)S(1)}, u32[]{:S(2)}, u32[]{:S(2)}) %collective-permute-start.3) | collective-permute-done | bytes 12320 | tf_op jit(solution)/shard_map/ppermute | solution.py:506
  15.1 0.0 collective-permute-done.4.rest_2_
  15.1 0.0 collective-permute-done.1.face_b
  15.1 0.0 collective-permute-done.face_a
  15.1 0.0 collective-permute-done.2.rest_0_
  15.1 0.4 %shard_map.50 = (f32[9,24,128]{2,1,0:T(8,128)S(1)}, f32[3,40,128]{2,1,0:T(8,128)S(1)}) custom-call(f32[9,16,128]{2,1,0:T(8,128)S(1)} %get-tuple-element.28.own, f32[9,2,16,128]{3,2,1,0:T(8,128)S(1)} %collective-permute-done.face_a, f32[9,2,16,128]{3,2,1,0:T(8,128)S(1)} %collective-permute-done.1.face_b, f32[9,8,8,128]{3,2,1,0:T(8,128)S(1)} %collective-permute-done.2.rest_0_, ...), custom_call_target="tpu_custom_call" | custom-call | flops 100000 | bytes 100000 | tf_op jit(solution)/shard_map/pallas_call | solution.py:476
  15.5 2.4 %collective-permute-start.5 = (f32[3,40,128]{2,1,0:T(8,128)S(1)}, f32[3,40,128]{2,1,0:T(8,128)S(1)}, u32[]{:S(2)}, u32[]{:S(2)}) collective-permute-start(f32[3,40,128]{2,1,0:T(8,128)S(1)} %get-tuple-element.30), channel_id=1, source_target_pairs={{0,3},{1,0},{2,1},{3,2},{4,7},{5,4},{6,5},{7,6},{8,11},{9,8},{10,9... | collective-permute-start | bytes 184328 | tf_op jit(solution)/shard_map/ppermute | solution.py:571
  17.8 1.9 %shard_map.49 = (f32[9,16,16,128]{3,2,1,0:T(8,128)S(1)}, f32[9,24,128]{2,1,0:T(8,128)S(1)}) custom-call(f32[9,16,16,128]{3,2,1,0:T(8,128)S(1)} %copy-done.1, f32[9,14,16,128]{3,2,1,0:T(8,128)S(1)} %get-tuple-element.19.part, f32[9,2,16,128]{3,2,1,0:T(8,128)S(1)} %get-tuple-element.20.outer, f32[9,16,128]{2,1,0:T(8,128)S(1)} %get-tuple-element.21.below, ...), custom_call_target="tpu_custom_call" | custom-call | flops 20000000 | bytes 20000000 | tf_op jit(solution)/shard_map/pallas_call | solution.py:476
  19.8 1.1 %collective-permute-done.5.above = f32[3,40,128]{2,1,0:T(8,128)S(1)} collective-permute-done((f32[3,40,128]{2,1,0:T(8,128)S(1)}, f32[3,40,128]{2,1,0:T(8,128)S(1)}, u32[]{:S(2)}, u32[]{:S(2)}) %collective-permute-start.5) | collective-permute-done | bytes 61472 | tf_op jit(solution)/shard_map/ppermute | solution.py:571
  20.8 1.4 %shard_map.51 = f32[9,16,16,128]{3,2,1,0:T(8,128)} custom-call(f32[9,16,16,128]{3,2,1,0:T(8,128)S(1)} %get-tuple-element.27.done, f32[9,24,128]{2,1,0:T(8,128)S(1)} %get-tuple-element.29.slab, f32[3,40,128]{2,1,0:T(8,128)S(1)} %collective-permute-done.5.above, f32[9,24,128]{2,1,0:T(8,128)S(1)} %get-tuple-element.31.lower, ...), custom_call_target="tpu_custom_call" | custom-call | flops 100000 | bytes 100000 | tf_op jit(solution)/shard_map/pallas_call | solution.py:476
Async XLA Ops:
  0.0 1.3 %copy-start = (f32[9,16,16,128]{3,2,1,0:T(8,128)S(1)}, f32[9,16,16,128]{3,2,1,0:T(8,128)}, u32[]{:S(2)}) copy-start(f32[9,16,16,128]{3,2,1,0:T(8,128)} %state.7) | copy-start | bytes 3538948
  1.3 9.0 %copy-start.4 = (s32[2,2,64,32]{2,3,1,0:T(8,128)S(1)}, s32[2,2,64,32]{2,3,1,0:T(8,128)}, u32[]{:S(2)}) copy-start(s32[2,2,64,32]{2,3,1,0:T(8,128)} %param.6) | copy-start | bytes 98308
  1.3 9.1 %copy-start.1 = (f32[9,16,16,128]{3,2,1,0:T(8,128)S(1)}, f32[9,16,16,128]{3,2,1,0:T(8,128)}, u32[]{:S(2)}) copy-start(f32[9,16,16,128]{3,2,1,0:T(8,128)} %state.7) | copy-start | bytes 3538948
  1.3 9.1 %copy-start.2 = (f32[8]{0:T(128)S(1)}, f32[8]{0:T(128)}, u32[]{:S(2)}) copy-start(f32[8]{0:T(128)} %mobility.1) | copy-start | bytes 100
  1.3 9.1 %copy-start.3 = (s32[2]{0:T(128)S(1)}, s32[2]{0:T(128)}, u32[]{:S(2)}) copy-start(s32[2]{0:T(128)} %shifts.1) | copy-start | bytes 28
  1.4 13.7 %collective-permute-start.2 = (f32[9,8,8,128]{3,2,1,0:T(8,128)S(1)}, f32[9,8,8,128]{3,2,1,0:T(8,128)S(1)}, u32[]{:S(2)}, u32[]{:S(2)}) collective-permute-start(f32[9,8,8,128]{3,2,1,0:T(8,128)S(1)} %get-tuple-element.24), channel_id=1, source_target_pairs={{0,4},{4,0},{1,5},{5,1},{2,6},{6,2},{3,7},{7,3},{8,12},{12,8},{9,1... | collective-permute-start | bytes 884744 | tf_op jit(solution)/shard_map/ppermute | solution.py:540
  4.4 10.7 %collective-permute-start.1 = (f32[9,2,16,128]{3,2,1,0:T(8,128)S(1)}, f32[9,2,16,128]{3,2,1,0:T(8,128)S(1)}, u32[]{:S(2)}, u32[]{:S(2)}) collective-permute-start(f32[9,2,16,128]{3,2,1,0:T(8,128)S(1)} %shard_map.48), channel_id=1, source_target_pairs={{8,16},{24,0},{16,8},{0,24},{9,17},{25,1},{17,9},{1,25},{10,18},{2... | collective-permute-start | bytes 442376 | tf_op jit(solution)/shard_map/ppermute | solution.py:500
  7.8 7.3 %collective-permute-start = (f32[9,2,16,128]{3,2,1,0:T(8,128)S(1)}, f32[9,2,16,128]{3,2,1,0:T(8,128)S(1)}, u32[]{:S(2)}, u32[]{:S(2)}) collective-permute-start(f32[9,2,16,128]{3,2,1,0:T(8,128)S(1)} %get-tuple-element.23), channel_id=1, source_target_pairs={{0,8},{16,24},{8,0},{24,16},{1,9},{17,25},{9,1},{25,17},{2,10},{18... | collective-permute-start | bytes 442376 | tf_op jit(solution)/shard_map/ppermute | solution.py:500
  7.8 7.3 %collective-permute-start.3 = (f32[3,8,128]{2,1,0:T(8,128)S(1)}, f32[3,8,128]{2,1,0:T(8,128)S(1)}, u32[]{:S(2)}, u32[]{:S(2)}) collective-permute-start(f32[3,8,128]{2,1,0:T(8,128)S(1)} %get-tuple-element.25), channel_id=1, source_target_pairs={{0,12},{4,8},{8,4},{12,0},{16,28},{20,24},{24,20},{28,16},{1,13},{... | collective-permute-start | bytes 36872 | tf_op jit(solution)/shard_map/ppermute | solution.py:506
  9.2 5.8 %collective-permute-start.4 = (f32[3,8,128]{2,1,0:T(8,128)S(1)}, f32[3,8,128]{2,1,0:T(8,128)S(1)}, u32[]{:S(2)}, u32[]{:S(2)}) collective-permute-start(f32[3,8,128]{2,1,0:T(8,128)S(1)} %get-tuple-element.26), channel_id=1, source_target_pairs={{0,28},{4,24},{8,20},{12,16},{16,12},{20,8},{24,4},{28,0},{1,29},{... | collective-permute-start | bytes 36872 | tf_op jit(solution)/shard_map/ppermute | solution.py:506
  15.5 5.4 %collective-permute-start.5 = (f32[3,40,128]{2,1,0:T(8,128)S(1)}, f32[3,40,128]{2,1,0:T(8,128)S(1)}, u32[]{:S(2)}, u32[]{:S(2)}) collective-permute-start(f32[3,40,128]{2,1,0:T(8,128)S(1)} %get-tuple-element.30), channel_id=1, source_target_pairs={{0,3},{1,0},{2,1},{3,2},{4,7},{5,4},{6,5},{7,6},{8,11},{9,8},{10,9... | collective-permute-start | bytes 184328 | tf_op jit(solution)/shard_map/ppermute | solution.py:571
